TPU v7x, 128 devices: a whole 4x4x4 slice. The times are simulated.
128 devices in a mesh: data: 1, dap2: 16 (over z, y), dap: 8 (over x, core).
Axes of the slice: x: 4, y: 4, z: 4, core: 2. Of those that a mesh axis runs over, the one named last changes fastest.
Arguments:
- pair_act: float32 [384, 384, 128], P(('data', 'dap'), 'dap2')
- pair_mask: int32 [384, 384], P(('data', 'dap'), 'dap2')
- ln_z: bfloat16 [16, 2, 2, 128], replicated
- w_ab: bfloat16 [16, 2, 128, 512], replicated
- w_g: bfloat16 [16, 2, 128, 128], replicated
- ln_x: bfloat16 [16, 2, 2, 128], replicated
- w_o: bfloat16 [16, 2, 128, 128], replicated
Outputs:
- output: float32 [384, 384, 128], P(('data', 'dap'), 'dap2')
All inputs are finite; a program needn't handle non-finite values.
Results may differ from a plain program's by a relative error of at most 0.00408477.
Values are sent between devices in bfloat16 or wider.
A program may use at most 1 GiB of HBM per device.

v0:
```python
import jax
import jax.numpy as jnp
from jax import lax
from jax.sharding import PartitionSpec as P

LN_EPS = 1e-5


def norm_last(values, params):
    mean = jnp.mean(values, axis=-1, keepdims=True)
    centered = values - mean
    variance = jnp.mean(centered * centered, axis=-1, keepdims=True)
    scaled = centered * lax.rsqrt(variance + LN_EPS)
    return (scaled * params[0].astype(jnp.float32) + params[1].astype(jnp.float32)).astype(jnp.bfloat16)


def norm_chan(values, params):
    mean = jnp.mean(values, axis=-3, keepdims=True)
    centered = values - mean
    variance = jnp.mean(centered * centered, axis=-3, keepdims=True)
    scaled = centered * lax.rsqrt(variance + LN_EPS)
    gain = params[0].astype(jnp.float32)[:, None, None]
    bias = params[1].astype(jnp.float32)[:, None, None]
    return (scaled * gain + bias).astype(jnp.bfloat16)


def project_local(z_norm, keep_mask, w_ab):
    hidden = w_ab.shape[1] // 4
    projected = jnp.einsum("ijd,de->eij", z_norm, w_ab, preferred_element_type=jnp.float32)
    a_proj = (keep_mask * jax.nn.sigmoid(projected[hidden:2 * hidden]) * projected[:hidden]).astype(jnp.bfloat16)
    b_proj = (keep_mask * jax.nn.sigmoid(projected[3 * hidden:]) * projected[2 * hidden:3 * hidden]).astype(jnp.bfloat16)
    return a_proj, b_proj


def finish_local(pair_state, z_norm, x_sum, ln_x, w_g, w_o):
    x_norm = norm_chan(x_sum, ln_x)
    update_val = jnp.einsum("cij,cd->ijd", x_norm, w_o, preferred_element_type=jnp.float32)
    gate_val = jax.nn.sigmoid(jnp.einsum("ijd,de->ije", z_norm, w_g, preferred_element_type=jnp.float32))
    return pair_state + gate_val * update_val


def to_transposed(blocks, row_devs, col_devs):
    hidden, n_rows, n_cols = blocks.shape
    n_full = n_rows * row_devs
    fine_rows = n_full // (row_devs * col_devs)
    stage_one = lax.all_to_all(blocks, "dap2", 1, 2, tiled=True)
    stage_one = stage_one.reshape(hidden, fine_rows, row_devs, col_devs * fine_rows)
    stage_two = lax.all_to_all(stage_one, "dap2", 3, 1, tiled=True)
    stage_three = lax.all_to_all(stage_two, "dap", 2, 1, tiled=True)
    stage_three = stage_three.reshape(hidden, n_full, fine_rows)
    return lax.all_to_all(stage_three, "dap2", 1, 2, tiled=True)


def solution(mesh):
    row_devs = mesh.shape["dap"]
    col_devs = mesh.shape["dap2"]
    pair_spec = P(("data", "dap"), "dap2", None)
    mask_spec = P(("data", "dap"), "dap2")

    def tri_update(pair_state, keep_mask, ln_z, w_ab, w_g, ln_x, w_o, outgoing):
        z_norm = norm_last(pair_state, ln_z)
        a_proj, b_proj = project_local(z_norm, keep_mask, w_ab)
        if outgoing:
            a_rows = lax.all_gather(a_proj, "dap2", axis=2, tiled=True)
            b_rows = lax.all_gather(to_transposed(b_proj, row_devs, col_devs), "dap", axis=2, tiled=True)
            x_sum = jnp.einsum("cik,cjk->cij", a_rows, b_rows, preferred_element_type=jnp.float32)
        else:
            a_cols = lax.all_gather(to_transposed(a_proj, row_devs, col_devs), "dap2", axis=1, tiled=True)
            b_cols = lax.all_gather(b_proj, "dap", axis=1, tiled=True)
            x_sum = jnp.einsum("cki,ckj->cij", a_cols, b_cols, preferred_element_type=jnp.float32)
        return finish_local(pair_state, z_norm, x_sum, ln_x, w_g, w_o)

    def local_stack(pair_act, pair_mask, ln_z, w_ab, w_g, ln_x, w_o):
        keep_mask = pair_mask.astype(jnp.float32)
        pair_state = pair_act
        for layer in range(w_o.shape[0]):
            pair_state = tri_update(pair_state, keep_mask, ln_z[layer, 0], w_ab[layer, 0], w_g[layer, 0], ln_x[layer, 0], w_o[layer, 0], True)
            pair_state = tri_update(pair_state, keep_mask, ln_z[layer, 1], w_ab[layer, 1], w_g[layer, 1], ln_x[layer, 1], w_o[layer, 1], False)
        return pair_state

    return jax.shard_map(local_stack, mesh=mesh, in_specs=(pair_spec, mask_spec, P(), P(), P(), P(), P()), out_specs=pair_spec, check_vma=False)
```

profile of v0, /device:TPU:0, one launch (start us, length us, event | category | flops | bytes accessed | tf_op | source)
XLA Modules:
  0.0 5328.2 jit_solution(17505389483149489058)
XLA Ops:
  72.2 18.8 all-gather.67.cloned.1.call-done
  95.7 56.6 %all-gather.65.cloned.1.call-done = bf16[128,48,384]{0,2,1:T(8,128)(2,1)} async-done(((bf16[128,48,24]{0,2,1:T(8,128)(2,1)}), bf16[128,48,384]{0,2,1:T(8,128)(2,1)}) %all-gather.65.cloned.1.call-update) | async-done | bytes 4718608 | tf_op jit(solution)/shard_map/all_gather | solution.py:64
  152.4 22.2 copy.1434
  247.9 86.6 %all-gather.69.cloned.1.call-done = bf16[128,384,48]{2,1,0:T(8,128)(2,1)} async-done(((bf16[128,24,48]{2,1,0:T(8,128)(2,1)}), bf16[128,384,48]{2,1,0:T(8,128)(2,1)}) %all-gather.69.cloned.1.call-update) | async-done | bytes 4718608 | tf_op jit(solution)/shard_map/all_gather | solution.py:68
  402.8 18.7 all-gather.75.cloned.1.call-done
  426.3 56.5 %all-gather.73.cloned.1.call-done = bf16[128,48,384]{0,2,1:T(8,128)(2,1)} async-done(((bf16[128,48,24]{0,2,1:T(8,128)(2,1)}), bf16[128,48,384]{0,2,1:T(8,128)(2,1)}) %all-gather.73.cloned.1.call-update) | async-done | bytes 4718608 | tf_op jit(solution)/shard_map/all_gather | solution.py:64
  482.8 22.2 copy.1466
  580.4 85.8 %all-gather.77.cloned.1.call-done = bf16[128,384,48]{2,1,0:T(8,128)(2,1)} async-done(((bf16[128,24,48]{2,1,0:T(8,128)(2,1)}), bf16[128,384,48]{2,1,0:T(8,128)(2,1)}) %all-gather.77.cloned.1.call-update) | async-done | bytes 4718608 | tf_op jit(solution)/shard_map/all_gather | solution.py:68
  733.7 19.6 all-gather.83.cloned.1.call-done
  758.0 56.5 %all-gather.81.cloned.1.call-done = bf16[128,48,384]{0,2,1:T(8,128)(2,1)} async-done(((bf16[128,48,24]{0,2,1:T(8,128)(2,1)}), bf16[128,48,384]{0,2,1:T(8,128)(2,1)}) %all-gather.81.cloned.1.call-update) | async-done | bytes 4718608 | tf_op jit(solution)/shard_map/all_gather | solution.py:64
  814.5 22.2 copy.1498
  911.6 86.3 %all-gather.85.cloned.1.call-done = bf16[128,384,48]{2,1,0:T(8,128)(2,1)} async-done(((bf16[128,24,48]{2,1,0:T(8,128)(2,1)}), bf16[128,384,48]{2,1,0:T(8,128)(2,1)}) %all-gather.85.cloned.1.call-update) | async-done | bytes 4718608 | tf_op jit(solution)/shard_map/all_gather | solution.py:68
  1065.7 19.3 all-gather.91.cloned.1.call-done
  1089.8 56.5 %all-gather.89.cloned.1.call-done = bf16[128,48,384]{0,2,1:T(8,128)(2,1)} async-done(((bf16[128,48,24]{0,2,1:T(8,128)(2,1)}), bf16[128,48,384]{0,2,1:T(8,128)(2,1)}) %all-gather.89.cloned.1.call-update) | async-done | bytes 4718608 | tf_op jit(solution)/shard_map/all_gather | solution.py:64
  1146.3 22.2 copy.1530
  1243.3 86.4 %all-gather.93.cloned.1.call-done = bf16[128,384,48]{2,1,0:T(8,128)(2,1)} async-done(((bf16[128,24,48]{2,1,0:T(8,128)(2,1)}), bf16[128,384,48]{2,1,0:T(8,128)(2,1)}) %all-gather.93.cloned.1.call-update) | async-done | bytes 4718608 | tf_op jit(solution)/shard_map/all_gather | solution.py:68
  1397.1 19.6 all-gather.99.cloned.1.call-done
  1421.5 56.5 %all-gather.97.cloned.1.call-done = bf16[128,48,384]{0,2,1:T(8,128)(2,1)} async-done(((bf16[128,48,24]{0,2,1:T(8,128)(2,1)}), bf16[128,48,384]{0,2,1:T(8,128)(2,1)}) %all-gather.97.cloned.1.call-update) | async-done | bytes 4718608 | tf_op jit(solution)/shard_map/all_gather | solution.py:64
  1478.0 22.2 copy.1562
  1575.1 86.3 %all-gather.101.cloned.1.call-done = bf16[128,384,48]{2,1,0:T(8,128)(2,1)} async-done(((bf16[128,24,48]{2,1,0:T(8,128)(2,1)}), bf16[128,384,48]{2,1,0:T(8,128)(2,1)}) %all-gather.101.cloned.1.call-update) | async-done | bytes 4718608 | tf_op jit(solution)/shard_map/all_gather | solution.py:68
  1729.3 19.2 all-gather.107.cloned.1.call-done
  1753.2 56.6 %all-gather.105.cloned.1.call-done = bf16[128,48,384]{0,2,1:T(8,128)(2,1)} async-done(((bf16[128,48,24]{0,2,1:T(8,128)(2,1)}), bf16[128,48,384]{0,2,1:T(8,128)(2,1)}) %all-gather.105.cloned.1.call-update) | async-done | bytes 4718608 | tf_op jit(solution)/shard_map/all_gather | solution.py:64
  1809.9 22.2 copy.1594
  1906.9 86.4 %all-gather.109.cloned.1.call-done = bf16[128,384,48]{2,1,0:T(8,128)(2,1)} async-done(((bf16[128,24,48]{2,1,0:T(8,128)(2,1)}), bf16[128,384,48]{2,1,0:T(8,128)(2,1)}) %all-gather.109.cloned.1.call-update) | async-done | bytes 4718608 | tf_op jit(solution)/shard_map/all_gather | solution.py:68
  2062.1 18.2 all-gather.115.cloned.1.call-done
  2085.1 56.5 %all-gather.113.cloned.1.call-done = bf16[128,48,384]{0,2,1:T(8,128)(2,1)} async-done(((bf16[128,48,24]{0,2,1:T(8,128)(2,1)}), bf16[128,48,384]{0,2,1:T(8,128)(2,1)}) %all-gather.113.cloned.1.call-update) | async-done | bytes 4718608 | tf_op jit(solution)/shard_map/all_gather | solution.py:64
  2141.6 22.2 copy.1626
  2237.3 86.5 %all-gather.117.cloned.1.call-done = bf16[128,384,48]{2,1,0:T(8,128)(2,1)} async-done(((bf16[128,24,48]{2,1,0:T(8,128)(2,1)}), bf16[128,384,48]{2,1,0:T(8,128)(2,1)}) %all-gather.117.cloned.1.call-update) | async-done | bytes 4718608 | tf_op jit(solution)/shard_map/all_gather | solution.py:68
  2394.0 18.5 all-gather.123.cloned.1.call-done
  2417.2 56.5 %all-gather.121.cloned.1.call-done = bf16[128,48,384]{0,2,1:T(8,128)(2,1)} async-done(((bf16[128,48,24]{0,2,1:T(8,128)(2,1)}), bf16[128,48,384]{0,2,1:T(8,128)(2,1)}) %all-gather.121.cloned.1.call-update) | async-done | bytes 4718608 | tf_op jit(solution)/shard_map/all_gather | solution.py:64
  2473.7 22.2 copy.1658
  2568.3 87.2 %all-gather.125.cloned.1.call-done = bf16[128,384,48]{2,1,0:T(8,128)(2,1)} async-done(((bf16[128,24,48]{2,1,0:T(8,128)(2,1)}), bf16[128,384,48]{2,1,0:T(8,128)(2,1)}) %all-gather.125.cloned.1.call-update) | async-done | bytes 4718608 | tf_op jit(solution)/shard_map/all_gather | solution.py:68
  2725.6 18.6 all-gather.131.cloned.1.call-done
  2748.9 56.7 %all-gather.129.cloned.1.call-done = bf16[128,48,384]{0,2,1:T(8,128)(2,1)} async-done(((bf16[128,48,24]{0,2,1:T(8,128)(2,1)}), bf16[128,48,384]{0,2,1:T(8,128)(2,1)}) %all-gather.129.cloned.1.call-update) | async-done | bytes 4718608 | tf_op jit(solution)/shard_map/all_gather | solution.py:64
  2805.6 22.2 copy.1690
  2900.3 87.1 %all-gather.133.cloned.1.call-done = bf16[128,384,48]{2,1,0:T(8,128)(2,1)} async-done(((bf16[128,24,48]{2,1,0:T(8,128)(2,1)}), bf16[128,384,48]{2,1,0:T(8,128)(2,1)}) %all-gather.133.cloned.1.call-update) | async-done | bytes 4718608 | tf_op jit(solution)/shard_map/all_gather | solution.py:68
  3057.7 18.3 all-gather.139.cloned.1.call-done
  3080.8 56.6 %all-gather.137.cloned.1.call-done = bf16[128,48,384]{0,2,1:T(8,128)(2,1)} async-done(((bf16[128,48,24]{0,2,1:T(8,128)(2,1)}), bf16[128,48,384]{0,2,1:T(8,128)(2,1)}) %all-gather.137.cloned.1.call-update) | async-done | bytes 4718608 | tf_op jit(solution)/shard_map/all_gather | solution.py:64
  3137.5 22.2 copy.1722
  3232.0 87.2 %all-gather.141.cloned.1.call-done = bf16[128,384,48]{2,1,0:T(8,128)(2,1)} async-done(((bf16[128,24,48]{2,1,0:T(8,128)(2,1)}), bf16[128,384,48]{2,1,0:T(8,128)(2,1)}) %all-gather.141.cloned.1.call-update) | async-done | bytes 4718608 | tf_op jit(solution)/shard_map/all_gather | solution.py:68
  3389.3 18.6 all-gather.147.cloned.1.call-done
  3412.7 56.7 %all-gather.145.cloned.1.call-done = bf16[128,48,384]{0,2,1:T(8,128)(2,1)} async-done(((bf16[128,48,24]{0,2,1:T(8,128)(2,1)}), bf16[128,48,384]{0,2,1:T(8,128)(2,1)}) %all-gather.145.cloned.1.call-update) | async-done | bytes 4718608 | tf_op jit(solution)/shard_map/all_gather | solution.py:64
  3469.3 22.2 copy.1754
  3565.3 85.8 %all-gather.149.cloned.1.call-done = bf16[128,384,48]{2,1,0:T(8,128)(2,1)} async-done(((bf16[128,24,48]{2,1,0:T(8,128)(2,1)}), bf16[128,384,48]{2,1,0:T(8,128)(2,1)}) %all-gather.149.cloned.1.call-update) | async-done | bytes 4718608 | tf_op jit(solution)/shard_map/all_gather | solution.py:68
  3719.4 18.8 all-gather.155.cloned.1.call-done
  3742.9 56.5 %all-gather.153.cloned.1.call-done = bf16[128,48,384]{0,2,1:T(8,128)(2,1)} async-done(((bf16[128,48,24]{0,2,1:T(8,128)(2,1)}), bf16[128,48,384]{0,2,1:T(8,128)(2,1)}) %all-gather.153.cloned.1.call-update) | async-done | bytes 4718608 | tf_op jit(solution)/shard_map/all_gather | solution.py:64
  3799.4 22.2 copy.1786
  3896.4 86.4 %all-gather.157.cloned.1.call-done = bf16[128,384,48]{2,1,0:T(8,128)(2,1)} async-done(((bf16[128,24,48]{2,1,0:T(8,128)(2,1)}), bf16[128,384,48]{2,1,0:T(8,128)(2,1)}) %all-gather.157.cloned.1.call-update) | async-done | bytes 4718608 | tf_op jit(solution)/shard_map/all_gather | solution.py:68
  4050.5 19.4 all-gather.163.cloned.1.call-done
  4074.6 56.6 %all-gather.161.cloned.1.call-done = bf16[128,48,384]{0,2,1:T(8,128)(2,1)} async-done(((bf16[128,48,24]{0,2,1:T(8,128)(2,1)}), bf16[128,48,384]{0,2,1:T(8,128)(2,1)}) %all-gather.161.cloned.1.call-update) | async-done | bytes 4718608 | tf_op jit(solution)/shard_map/all_gather | solution.py:64
  4131.3 22.2 copy.1818
  4228.4 86.3 %all-gather.165.cloned.1.call-done = bf16[128,384,48]{2,1,0:T(8,128)(2,1)} async-done(((bf16[128,24,48]{2,1,0:T(8,128)(2,1)}), bf16[128,384,48]{2,1,0:T(8,128)(2,1)}) %all-gather.165.cloned.1.call-update) | async-done | bytes 4718608 | tf_op jit(solution)/shard_map/all_gather | solution.py:68
  4382.6 19.2 all-gather.171.cloned.1.call-done
  4406.5 56.7 %all-gather.169.cloned.1.call-done = bf16[128,48,384]{0,2,1:T(8,128)(2,1)} async-done(((bf16[128,48,24]{0,2,1:T(8,128)(2,1)}), bf16[128,48,384]{0,2,1:T(8,128)(2,1)}) %all-gather.169.cloned.1.call-update) | async-done | bytes 4718608 | tf_op jit(solution)/shard_map/all_gather | solution.py:64
  4463.2 22.2 copy.1850
  4560.2 86.4 %all-gather.173.cloned.1.call-done = bf16[128,384,48]{2,1,0:T(8,128)(2,1)} async-done(((bf16[128,24,48]{2,1,0:T(8,128)(2,1)}), bf16[128,384,48]{2,1,0:T(8,128)(2,1)}) %all-gather.173.cloned.1.call-update) | async-done | bytes 4718608 | tf_op jit(solution)/shard_map/all_gather | solution.py:68
  4714.1 19.6 all-gather.179.cloned.1.call-done
  4738.4 56.5 %all-gather.177.cloned.1.call-done = bf16[128,48,384]{0,2,1:T(8,128)(2,1)} async-done(((bf16[128,48,24]{0,2,1:T(8,128)(2,1)}), bf16[128,48,384]{0,2,1:T(8,128)(2,1)}) %all-gather.177.cloned.1.call-update) | async-done | bytes 4718608 | tf_op jit(solution)/shard_map/all_gather | solution.py:64
  4794.9 22.2 copy.1882
  4892.0 86.3 %all-gather.181.cloned.1.call-done = bf16[128,384,48]{2,1,0:T(8,128)(2,1)} async-done(((bf16[128,24,48]{2,1,0:T(8,128)(2,1)}), bf16[128,384,48]{2,1,0:T(8,128)(2,1)}) %all-gather.181.cloned.1.call-update) | async-done | bytes 4718608 | tf_op jit(solution)/shard_map/all_gather | solution.py:68
  5046.2 19.2 all-gather.187.cloned.1.call-done
  5070.1 56.7 %all-gather.185.cloned.1.call-done = bf16[128,48,384]{0,2,1:T(8,128)(2,1)} async-done(((bf16[128,48,24]{0,2,1:T(8,128)(2,1)}), bf16[128,48,384]{0,2,1:T(8,128)(2,1)}) %all-gather.185.cloned.1.call-update) | async-done | bytes 4718608 | tf_op jit(solution)/shard_map/all_gather | solution.py:64
  5126.8 22.2 copy.1914
  5223.0 87.2 %all-gather.189.cloned.1.call-done = bf16[128,384,48]{2,1,0:T(8,128)(2,1)} async-done(((bf16[128,24,48]{2,1,0:T(8,128)(2,1)}), bf16[128,384,48]{2,1,0:T(8,128)(2,1)}) %all-gather.189.cloned.1.call-update) | async-done | bytes 4718608 | tf_op jit(solution)/shard_map/all_gather | solution.py:68
  (1157 shorter events, 2362.0 us)
Async XLA Ops:
  6.5 84.4 %all-gather.67.cloned.1.call-start = ((), (), s32[]{:S(2)}) async-start(), calls=%async_computation.129 | async-start | bytes 2654208 | tf_op jit(solution)/shard_map/all_gather | solution.py:65
  69.2 83.1 %all-gather.65.cloned.1.call-start = ((), (), s32[]{:S(2)}) async-start(), calls=%async_computation.128 | async-start | bytes 5013504 | tf_op jit(solution)/shard_map/all_gather | solution.py:64
  70.0 173.1 %all-gather.71.cloned.1.call-start = ((), (), s32[]{:S(2)}) async-start(), calls=%async_computation.131 | async-start | bytes 2654208 | tf_op jit(solution)/shard_map/all_gather | solution.py:69
  188.1 146.3 %all-gather.69.cloned.1.call-start = ((), (), s32[]{:S(2)}) async-start(), calls=%async_computation.130 | async-start | bytes 13369344 | tf_op jit(solution)/shard_map/all_gather | solution.py:68
  240.9 180.6 %all-gather.75.cloned.1.call-start = ((), (), s32[]{:S(2)}) async-start(), calls=%async_computation.133 | async-start | bytes 2654208 | tf_op jit(solution)/shard_map/all_gather | solution.py:65
  399.8 83.0 %all-gather.73.cloned.1.call-start = ((), (), s32[]{:S(2)}) async-start(), calls=%async_computation.132 | async-start | bytes 5013504 | tf_op jit(solution)/shard_map/all_gather | solution.py:64
  400.4 175.2 %all-gather.79.cloned.1.call-start = ((), (), s32[]{:S(2)}) async-start(), calls=%async_computation.135 | async-start | bytes 2654208 | tf_op jit(solution)/shard_map/all_gather | solution.py:69
  520.2 146.0 %all-gather.77.cloned.1.call-start = ((), (), s32[]{:S(2)}) async-start(), calls=%async_computation.134 | async-start | bytes 13369344 | tf_op jit(solution)/shard_map/all_gather | solution.py:68
  572.7 180.6 %all-gather.83.cloned.1.call-start = ((), (), s32[]{:S(2)}) async-start(), calls=%async_computation.137 | async-start | bytes 2654208 | tf_op jit(solution)/shard_map/all_gather | solution.py:65
  731.5 83.0 %all-gather.81.cloned.1.call-start = ((), (), s32[]{:S(2)}) async-start(), calls=%async_computation.136 | async-start | bytes 5013504 | tf_op jit(solution)/shard_map/all_gather | solution.py:64
  732.1 174.7 %all-gather.87.cloned.1.call-start = ((), (), s32[]{:S(2)}) async-start(), calls=%async_computation.139 | async-start | bytes 2654208 | tf_op jit(solution)/shard_map/all_gather | solution.py:69
  851.9 146.0 %all-gather.85.cloned.1.call-start = ((), (), s32[]{:S(2)}) async-start(), calls=%async_computation.138 | async-start | bytes 13369344 | tf_op jit(solution)/shard_map/all_gather | solution.py:68
  904.4 180.6 %all-gather.91.cloned.1.call-start = ((), (), s32[]{:S(2)}) async-start(), calls=%async_computation.141 | async-start | bytes 2654208 | tf_op jit(solution)/shard_map/all_gather | solution.py:65
  1063.2 83.0 %all-gather.89.cloned.1.call-start = ((), (), s32[]{:S(2)}) async-start(), calls=%async_computation.140 | async-start | bytes 5013504 | tf_op jit(solution)/shard_map/all_gather | solution.py:64
  1063.8 174.6 %all-gather.95.cloned.1.call-start = ((), (), s32[]{:S(2)}) async-start(), calls=%async_computation.143 | async-start | bytes 2654208 | tf_op jit(solution)/shard_map/all_gather | solution.py:69
  1183.7 146.0 %all-gather.93.cloned.1.call-start = ((), (), s32[]{:S(2)}) async-start(), calls=%async_computation.142 | async-start | bytes 13369344 | tf_op jit(solution)/shard_map/all_gather | solution.py:68
  1236.1 180.6 %all-gather.99.cloned.1.call-start = ((), (), s32[]{:S(2)}) async-start(), calls=%async_computation.145 | async-start | bytes 2654208 | tf_op jit(solution)/shard_map/all_gather | solution.py:65
  1395.0 83.0 %all-gather.97.cloned.1.call-start = ((), (), s32[]{:S(2)}) async-start(), calls=%async_computation.144 | async-start | bytes 5013504 | tf_op jit(solution)/shard_map/all_gather | solution.py:64
  1395.6 174.7 %all-gather.103.cloned.1.call-start = ((), (), s32[]{:S(2)}) async-start(), calls=%async_computation.147 | async-start | bytes 2654208 | tf_op jit(solution)/shard_map/all_gather | solution.py:69
  1515.4 146.0 %all-gather.101.cloned.1.call-start = ((), (), s32[]{:S(2)}) async-start(), calls=%async_computation.146 | async-start | bytes 13369344 | tf_op jit(solution)/shard_map/all_gather | solution.py:68
  1567.9 180.6 %all-gather.107.cloned.1.call-start = ((), (), s32[]{:S(2)}) async-start(), calls=%async_computation.149 | async-start | bytes 2654208 | tf_op jit(solution)/shard_map/all_gather | solution.py:65
  1726.7 83.1 %all-gather.105.cloned.1.call-start = ((), (), s32[]{:S(2)}) async-start(), calls=%async_computation.148 | async-start | bytes 5013504 | tf_op jit(solution)/shard_map/all_gather | solution.py:64
  1727.5 174.6 %all-gather.111.cloned.1.call-start = ((), (), s32[]{:S(2)}) async-start(), calls=%async_computation.151 | async-start | bytes 2654208 | tf_op jit(solution)/shard_map/all_gather | solution.py:69
  1847.3 146.0 %all-gather.109.cloned.1.call-start = ((), (), s32[]{:S(2)}) async-start(), calls=%async_computation.150 | async-start | bytes 13369344 | tf_op jit(solution)/shard_map/all_gather | solution.py:68
  1899.7 180.6 %all-gather.115.cloned.1.call-start = ((), (), s32[]{:S(2)}) async-start(), calls=%async_computation.153 | async-start | bytes 2654208 | tf_op jit(solution)/shard_map/all_gather | solution.py:65
  2058.6 83.0 %all-gather.113.cloned.1.call-start = ((), (), s32[]{:S(2)}) async-start(), calls=%async_computation.152 | async-start | bytes 5013504 | tf_op jit(solution)/shard_map/all_gather | solution.py:64
  2059.2 173.2 %all-gather.119.cloned.1.call-start = ((), (), s32[]{:S(2)}) async-start(), calls=%async_computation.155 | async-start | bytes 2654208 | tf_op jit(solution)/shard_map/all_gather | solution.py:69
  2177.8 146.0 %all-gather.117.cloned.1.call-start = ((), (), s32[]{:S(2)}) async-start(), calls=%async_computation.154 | async-start | bytes 13369344 | tf_op jit(solution)/shard_map/all_gather | solution.py:68
  2230.2 182.2 %all-gather.123.cloned.1.call-start = ((), (), s32[]{:S(2)}) async-start(), calls=%async_computation.157 | async-start | bytes 2654208 | tf_op jit(solution)/shard_map/all_gather | solution.py:65
  2390.7 83.0 %all-gather.121.cloned.1.call-start = ((), (), s32[]{:S(2)}) async-start(), calls=%async_computation.156 | async-start | bytes 5013504 | tf_op jit(solution)/shard_map/all_gather | solution.py:64
  2391.3 172.2 %all-gather.127.cloned.1.call-start = ((), (), s32[]{:S(2)}) async-start(), calls=%async_computation.159 | async-start | bytes 2654208 | tf_op jit(solution)/shard_map/all_gather | solution.py:69
  2509.5 146.0 %all-gather.125.cloned.1.call-start = ((), (), s32[]{:S(2)}) async-start(), calls=%async_computation.158 | async-start | bytes 13369344 | tf_op jit(solution)/shard_map/all_gather | solution.py:68
  2561.9 182.2 %all-gather.131.cloned.1.call-start = ((), (), s32[]{:S(2)}) async-start(), calls=%async_computation.161 | async-start | bytes 2654208 | tf_op jit(solution)/shard_map/all_gather | solution.py:65
  2722.4 83.2 %all-gather.129.cloned.1.call-start = ((), (), s32[]{:S(2)}) async-start(), calls=%async_computation.160 | async-start | bytes 5013504 | tf_op jit(solution)/shard_map/all_gather | solution.py:64
  2723.2 172.3 %all-gather.135.cloned.1.call-start = ((), (), s32[]{:S(2)}) async-start(), calls=%async_computation.163 | async-start | bytes 2654208 | tf_op jit(solution)/shard_map/all_gather | solution.py:69
  2841.3 146.0 %all-gather.133.cloned.1.call-start = ((), (), s32[]{:S(2)}) async-start(), calls=%async_computation.162 | async-start | bytes 13369344 | tf_op jit(solution)/shard_map/all_gather | solution.py:68
  2893.8 182.2 %all-gather.139.cloned.1.call-start = ((), (), s32[]{:S(2)}) async-start(), calls=%async_computation.165 | async-start | bytes 2654208 | tf_op jit(solution)/shard_map/all_gather | solution.py:65
  3054.3 83.1 %all-gather.137.cloned.1.call-start = ((), (), s32[]{:S(2)}) async-start(), calls=%async_computation.164 | async-start | bytes 5013504 | tf_op jit(solution)/shard_map/all_gather | solution.py:64
  3055.1 172.2 %all-gather.143.cloned.1.call-start = ((), (), s32[]{:S(2)}) async-start(), calls=%async_computation.167 | async-start | bytes 2654208 | tf_op jit(solution)/shard_map/all_gather | solution.py:69
  3173.2 146.0 %all-gather.141.cloned.1.call-start = ((), (), s32[]{:S(2)}) async-start(), calls=%async_computation.166 | async-start | bytes 13369344 | tf_op jit(solution)/shard_map/all_gather | solution.py:68
  3225.7 182.2 %all-gather.147.cloned.1.call-start = ((), (), s32[]{:S(2)}) async-start(), calls=%async_computation.169 | async-start | bytes 2654208 | tf_op jit(solution)/shard_map/all_gather | solution.py:65
  3386.2 83.2 %all-gather.145.cloned.1.call-start = ((), (), s32[]{:S(2)}) async-start(), calls=%async_computation.168 | async-start | bytes 5013504 | tf_op jit(solution)/shard_map/all_gather | solution.py:64
  3386.9 173.6 %all-gather.151.cloned.1.call-start = ((), (), s32[]{:S(2)}) async-start(), calls=%async_computation.171 | async-start | bytes 2654208 | tf_op jit(solution)/shard_map/all_gather | solution.py:69
  3505.1 146.0 %all-gather.149.cloned.1.call-start = ((), (), s32[]{:S(2)}) async-start(), calls=%async_computation.170 | async-start | bytes 13369344 | tf_op jit(solution)/shard_map/all_gather | solution.py:68
  3557.6 180.6 %all-gather.155.cloned.1.call-start = ((), (), s32[]{:S(2)}) async-start(), calls=%async_computation.173 | async-start | bytes 2654208 | tf_op jit(solution)/shard_map/all_gather | solution.py:65
  3716.4 83.0 %all-gather.153.cloned.1.call-start = ((), (), s32[]{:S(2)}) async-start(), calls=%async_computation.172 | async-start | bytes 5013504 | tf_op jit(solution)/shard_map/all_gather | solution.py:64
  3717.0 174.6 %all-gather.159.cloned.1.call-start = ((), (), s32[]{:S(2)}) async-start(), calls=%async_computation.175 | async-start | bytes 2654208 | tf_op jit(solution)/shard_map/all_gather | solution.py:69
  3836.8 146.0 %all-gather.157.cloned.1.call-start = ((), (), s32[]{:S(2)}) async-start(), calls=%async_computation.174 | async-start | bytes 13369344 | tf_op jit(solution)/shard_map/all_gather | solution.py:68
  3889.3 180.6 %all-gather.163.cloned.1.call-start = ((), (), s32[]{:S(2)}) async-start(), calls=%async_computation.177 | async-start | bytes 2654208 | tf_op jit(solution)/shard_map/all_gather | solution.py:65
  4048.1 83.1 %all-gather.161.cloned.1.call-start = ((), (), s32[]{:S(2)}) async-start(), calls=%async_computation.176 | async-start | bytes 5013504 | tf_op jit(solution)/shard_map/all_gather | solution.py:64
  4048.9 174.7 %all-gather.167.cloned.1.call-start = ((), (), s32[]{:S(2)}) async-start(), calls=%async_computation.179 | async-start | bytes 2654208 | tf_op jit(solution)/shard_map/all_gather | solution.py:69
  4168.7 146.0 %all-gather.165.cloned.1.call-start = ((), (), s32[]{:S(2)}) async-start(), calls=%async_computation.178 | async-start | bytes 13369344 | tf_op jit(solution)/shard_map/all_gather | solution.py:68
  4221.2 180.6 %all-gather.171.cloned.1.call-start = ((), (), s32[]{:S(2)}) async-start(), calls=%async_computation.181 | async-start | bytes 2654208 | tf_op jit(solution)/shard_map/all_gather | solution.py:65
  4380.0 83.2 %all-gather.169.cloned.1.call-start = ((), (), s32[]{:S(2)}) async-start(), calls=%async_computation.180 | async-start | bytes 5013504 | tf_op jit(solution)/shard_map/all_gather | solution.py:64
  4380.8 174.6 %all-gather.175.cloned.1.call-start = ((), (), s32[]{:S(2)}) async-start(), calls=%async_computation.183 | async-start | bytes 2654208 | tf_op jit(solution)/shard_map/all_gather | solution.py:69
  4500.6 146.0 %all-gather.173.cloned.1.call-start = ((), (), s32[]{:S(2)}) async-start(), calls=%async_computation.182 | async-start | bytes 13369344 | tf_op jit(solution)/shard_map/all_gather | solution.py:68
  4553.1 180.6 %all-gather.179.cloned.1.call-start = ((), (), s32[]{:S(2)}) async-start(), calls=%async_computation.185 | async-start | bytes 2654208 | tf_op jit(solution)/shard_map/all_gather | solution.py:65
  4711.9 83.0 %all-gather.177.cloned.1.call-start = ((), (), s32[]{:S(2)}) async-start(), calls=%async_computation.184 | async-start | bytes 5013504 | tf_op jit(solution)/shard_map/all_gather | solution.py:64
  4712.5 174.7 %all-gather.183.cloned.1.call-start = ((), (), s32[]{:S(2)}) async-start(), calls=%async_computation.187 | async-start | bytes 2654208 | tf_op jit(solution)/shard_map/all_gather | solution.py:69
  4832.3 146.0 %all-gather.181.cloned.1.call-start = ((), (), s32[]{:S(2)}) async-start(), calls=%async_computation.186 | async-start | bytes 13369344 | tf_op jit(solution)/shard_map/all_gather | solution.py:68
  4884.8 180.6 %all-gather.187.cloned.1.call-start = ((), (), s32[]{:S(2)}) async-start(), calls=%async_computation.189 | async-start | bytes 2654208 | tf_op jit(solution)/shard_map/all_gather | solution.py:65
  5043.6 83.2 %all-gather.185.cloned.1.call-start = ((), (), s32[]{:S(2)}) async-start(), calls=%async_computation.188 | async-start | bytes 5013504 | tf_op jit(solution)/shard_map/all_gather | solution.py:64
  5044.4 173.8 %all-gather.191.cloned.1.call-start = ((), (), s32[]{:S(2)}) async-start(), calls=%async_computation.191 | async-start | bytes 2654208 | tf_op jit(solution)/shard_map/all_gather | solution.py:69
  5164.2 146.0 %all-gather.189.cloned.1.call-start = ((), (), s32[]{:S(2)}) async-start(), calls=%async_computation.190 | async-start | bytes 13369344 | tf_op jit(solution)/shard_map/all_gather | solution.py:68
  (13 other events, 62.6 us)
Sparse Core Ops, SparseCore 0:
  69.4 21.5 all-gather.66
  93.1 59.2 all-gather.64
  188.3 24.9 all-gather.70
  241.0 93.4 all-gather.68
  399.9 21.5 all-gather.74
  423.5 59.2 all-gather.72
  520.3 24.9 all-gather.78
  572.8 93.4 all-gather.76
  731.6 21.5 all-gather.82
  755.2 59.2 all-gather.80
  852.0 24.9 all-gather.86
  904.5 93.4 all-gather.84
  1063.4 21.5 all-gather.90
  1086.9 59.2 all-gather.88
  1183.8 24.9 all-gather.94
  1236.2 93.4 all-gather.92
  1395.1 21.5 all-gather.98
  1418.7 59.2 all-gather.96
  1515.5 24.9 all-gather.102
  1568.0 93.4 all-gather.100
  1726.8 21.5 all-gather.106
  1750.6 59.2 all-gather.104
  1847.4 24.9 all-gather.110
  1899.9 93.4 all-gather.108
  2058.8 21.5 all-gather.114
  2082.3 59.2 all-gather.112
  2177.9 24.9 all-gather.118
  2230.4 93.4 all-gather.116
  2390.8 21.5 all-gather.122
  2414.4 59.2 all-gather.120
  2509.6 24.9 all-gather.126
  2562.1 93.4 all-gather.124
  2722.6 21.5 all-gather.130
  2746.3 59.2 all-gather.128
  2841.5 24.9 all-gather.134
  2893.9 93.4 all-gather.132
  3054.4 21.5 all-gather.138
  3078.1 59.2 all-gather.136
  3173.3 24.9 all-gather.142
  3225.8 93.4 all-gather.140
  3386.3 21.5 all-gather.146
  3410.0 59.2 all-gather.144
  3505.2 24.9 all-gather.150
  3557.7 93.4 all-gather.148
  3716.5 21.5 all-gather.154
  3740.1 59.2 all-gather.152
  3836.9 24.9 all-gather.158
  3889.4 93.4 all-gather.156
  4048.3 21.5 all-gather.162
  4072.0 59.2 all-gather.160
  4168.8 24.9 all-gather.166
  4221.3 93.4 all-gather.164
  4380.1 21.5 all-gather.170
  4403.9 59.2 all-gather.168
  4500.7 24.9 all-gather.174
  4553.2 93.4 all-gather.172
  4712.0 21.5 all-gather.178
  4735.6 59.2 all-gather.176
  4832.4 24.9 all-gather.182
  4884.9 93.4 all-gather.180
  5043.8 21.5 all-gather.186
  5067.5 59.2 all-gather.184
  5164.3 24.9 all-gather.190
  5217.0 93.2 all-gather.188
where the time goes:
time: 5350 us; the launch traced here: 5330 us
  waiting for transfers between devices  2600 us (49%)
  blocking collectives  1620 us (30%)
  local copies, waits for them, and re-layouts  602 us (11%)
  matrix products  387 us (7%)
  other arithmetic  87.9 us (2%)
    all_gather x16, waiting for transfers between devices, tri_update(): lax.all_gather(to_transposed(a_proj, row_devs, col_devs), 'dap2', axis=1,...  1380 us
    all_gather x16, waiting for transfers between devices, tri_update(): a_rows = lax.all_gather(a_proj, 'dap2', axis=2, tiled=True)  905 us
    all_to_all x32, blocking collectives, to_transposed(): stage_one = lax.all_to_all(blocks, 'dap2', 1, 2, tiled=True)  439 us
    all_to_all x32, blocking collectives, to_transposed(): return lax.all_to_all(stage_three, 'dap2', 1, 2, tiled=True)  419 us
    all_to_all x32, blocking collectives, to_transposed(): stage_three = lax.all_to_all(stage_two, 'dap', 2, 1, tiled=True)  386 us
    all_to_all x32, blocking collectives, to_transposed(): stage_two = lax.all_to_all(stage_one, 'dap2', 3, 1, tiled=True)  375 us
    all_gather x16, local copies, waits for them, and re-layouts, tri_update(): a_rows = lax.all_gather(a_proj, 'dap2', axis=2, tiled=True)  355 us
    all_gather x16, waiting for transfers between devices, tri_update(): lax.all_gather(to_transposed(b_proj, row_devs, col_devs), 'dap', axis=2,...  303 us
  transfers between devices with their start and end apart: 64, of which 48 were waited for; matrix products, arithmetic and copies ran while one was open for 5% of the time, Pallas kernels for 0%

commit v1 on v0

v1 whole, which is shorter than its diff:
```python
import functools

import jax
import jax.numpy as jnp
from jax import lax
from jax.experimental import pallas as pl
from jax.experimental.pallas import tpu as pltpu
from jax.sharding import PartitionSpec as P

LN_EPS = 1e-5
N_DEV = 128
CH = 128
N = 384
R = 3
MESH = pl.DeviceIdType.MESH


def norm_cols(v, gain, bias):
    mean = jnp.mean(v, axis=0, keepdims=True)
    cen = v - mean
    var = jnp.mean(cen * cen, axis=0, keepdims=True)
    return (cen * lax.rsqrt(var + LN_EPS) * gain + bias).astype(jnp.bfloat16)


def body(n_layers, z_in, mask, w_in, w_out, lnp, z_ref,
         s_ab, r_ab, s_x, r_x, stage, stage2, a_mat, b_mat, xn_buf,
         sem_sab, sem_rab, sem_sx, sem_rx):
    d2 = lax.axis_index("dap2")
    d1 = lax.axis_index("dap")
    cz, cy = d2 // 4, d2 % 4
    cx, cc = d1 // 2, d1 % 2
    me = d1 * 16 + d2
    cols = [((cx + dx) % 4) * 2 + (cc + dc) % 2 for dx in (2, 1, 3, 0) for dc in (1, 0)]

    def all_peers(fn):
        def one(q, carry):
            dz, dy = (4 - q // 4 + 3) % 4, (4 - q % 4 + 3) % 4
            t2 = ((cz + dz) % 4) * 4 + (cy + dy) % 4
            for i, t1 in enumerate(cols):
                if i == 7:
                    @pl.when(q != 15)
                    def _():
                        fn(t2, t1)
                else:
                    fn(t2, t1)
            return carry
        lax.fori_loop(0, 16, one, 0)

    bar = pltpu.get_barrier_semaphore()
    all_peers(lambda t2, t1: pl.semaphore_signal(bar, inc=1, device_id=(0, t2, t1), device_id_type=MESH))
    pl.semaphore_wait(bar, N_DEV - 1)

    z_ref[...] = z_in[...]

    def send(src, dst, rows, sem_s, sem_r, r):
        def one(t2, t1):
            t = t1 * 16 + t2
            pltpu.make_async_remote_copy(
                src_ref=src.at[r, pl.ds(t * rows, rows)], dst_ref=dst.at[r, pl.ds(me * rows, rows)],
                send_sem=sem_s.at[r], recv_sem=sem_r.at[r], device_id=(0, t2, t1), device_id_type=MESH).start()
        all_peers(one)

    def wait(src, dst, rows, sem, r):
        part = pl.ds(0, rows * (N_DEV - 1))
        pltpu.make_async_copy(src.at[r, part], dst.at[r, part], sem.at[r]).wait()

    def project(u, r, first):
        tok = pl.ds(r * N, N)
        zn = norm_cols(z_ref[:, tok], lnp[u, :, 0:1], lnp[u, :, 1:2])
        q = jnp.dot(w_in[u], zn, preferred_element_type=jnp.float32)
        m = mask[:, tok]
        a = m * jax.nn.sigmoid(q[CH:2 * CH]) * q[:CH]
        b = m * jax.nn.sigmoid(q[3 * CH:4 * CH]) * q[2 * CH:3 * CH]
        xn_buf[:, tok] = jax.nn.sigmoid(q[4 * CH:])
        for kh in range(3):
            stage[pl.ds(2 * kh, CH, stride=6), :] = a[:, kh * 128:(kh + 1) * 128]
            stage[pl.ds(2 * kh + 1, CH, stride=6), :] = b[:, kh * 128:(kh + 1) * 128]
        if not first:
            wait(s_ab, r_ab, 6, sem_sab, r)
        s_ab[r] = stage[...].astype(jnp.bfloat16)
        send(s_ab, r_ab, 6, sem_sab, sem_rab, r)

    def gather_mats(r):
        wait(s_ab, r_ab, 6, sem_rab, r)
        stage[...] = r_ab[r].astype(jnp.float32)
        stage2[...] = s_ab[r].astype(jnp.float32)
        stage[pl.ds(6 * me, 6), :] = stage2[pl.ds(6 * me, 6), :]
        for kh in range(3):
            a_mat[r * 128:(r + 1) * 128, kh * 128:(kh + 1) * 128] = stage[pl.ds(2 * kh, 128, stride=6), :].astype(jnp.bfloat16)
            b_mat[r * 128:(r + 1) * 128, kh * 128:(kh + 1) * 128] = stage[pl.ds(2 * kh + 1, 128, stride=6), :].astype(jnp.bfloat16)

    def contract(outgoing, r):
        if outgoing:
            x = lax.dot_general(a_mat[r * 128:(r + 1) * 128, :], b_mat[...], (((1,), (1,)), ((), ())),
                                preferred_element_type=jnp.float32)
        else:
            x = lax.dot_general(a_mat[:, r * 128:(r + 1) * 128], b_mat[...], (((0,), (0,)), ((), ())),
                                preferred_element_type=jnp.float32)
        for jh in range(3):
            s_x[r, pl.ds(jh, 128, stride=3), :] = x[:, jh * 128:(jh + 1) * 128]
        send(s_x, r_x, 3, sem_sx, sem_rx, r)

    def finish(u, r):
        wait(s_x, r_x, 3, sem_rx, r)
        r_x[r, pl.ds(3 * me, 3), :] = s_x[r, pl.ds(3 * me, 3), :]
        for jh in range(3):
            tok = slice(r * N + jh * 128, r * N + (jh + 1) * 128)
            x = r_x[r, pl.ds(jh, CH, stride=3), :]
            xn = norm_cols(x, lnp[u, :, 2:3], lnp[u, :, 3:4])
            y = jnp.dot(w_out[u], xn, preferred_element_type=jnp.float32)
            z_ref[:, tok] = z_ref[:, tok] + xn_buf[:, tok] * y
        wait(s_x, r_x, 3, sem_sx, r)

    def update(u, outgoing):
        for r in range(R):
            gather_mats(r)
        for r in range(R):
            contract(outgoing, r)
        for r in range(R):
            finish(u, r)

    for r in range(R):
        project(0, r, True)

    def layer(l, carry):
        update(2 * l, True)
        for r in range(R):
            project(2 * l + 1, r, False)
        update(2 * l + 1, False)

        @pl.when(l < n_layers - 1)
        def _():
            for r in range(R):
                project(2 * l + 2, r, False)
        return carry

    lax.fori_loop(0, n_layers, layer, 0)
    for r in range(R):
        wait(s_ab, r_ab, 6, sem_sab, r)


def solution(mesh):
    pair_spec = P(("data", "dap"), "dap2", None)
    mask_spec = P(("data", "dap"), "dap2")

    def local_stack(pair_act, pair_mask, ln_z, w_ab, w_g, ln_x, w_o):
        n_layers = w_o.shape[0]
        z = lax.all_to_all(pair_act, "dap2", 0, 1, tiled=True)
        z = z.reshape(R, N_DEV, R, CH).transpose(3, 0, 2, 1).reshape(CH, R * N)
        m = lax.all_to_all(pair_mask, "dap2", 0, 1, tiled=True)
        m = m.reshape(R, N_DEV, R).transpose(0, 2, 1).reshape(1, R * N).astype(jnp.float32)
        w_in = jnp.concatenate([w_ab, w_g], axis=-1).transpose(0, 1, 3, 2).reshape(2 * n_layers, 5 * CH, CH)
        w_out = w_o.transpose(0, 1, 3, 2).reshape(2 * n_layers, CH, CH)
        lnp = jnp.stack([ln_z[:, :, 0], ln_z[:, :, 1], ln_x[:, :, 0], ln_x[:, :, 1]], axis=-1)
        lnp = lnp.astype(jnp.float32).reshape(2 * n_layers, CH, 4)
        vmem = pl.BlockSpec(memory_space=pltpu.VMEM)
        dma = pltpu.SemaphoreType.DMA((R,))
        z = pl.pallas_call(
            functools.partial(body, n_layers),
            out_shape=jax.ShapeDtypeStruct((CH, R * N), jnp.float32),
            in_specs=[vmem] * 5, out_specs=vmem,
            scratch_shapes=[
                pltpu.VMEM((R, 6 * N_DEV, 128), jnp.bfloat16), pltpu.VMEM((R, 6 * N_DEV, 128), jnp.bfloat16),
                pltpu.VMEM((R, 3 * N_DEV, 128), jnp.float32), pltpu.VMEM((R, 3 * N_DEV, 128), jnp.float32),
                pltpu.VMEM((6 * N_DEV, 128), jnp.float32), pltpu.VMEM((6 * N_DEV, 128), jnp.float32),
                pltpu.VMEM((N, N), jnp.bfloat16), pltpu.VMEM((N, N), jnp.bfloat16),
                pltpu.VMEM((CH, R * N), jnp.float32), dma, dma, dma, dma],
            compiler_params=pltpu.CompilerParams(collective_id=0, has_side_effects=True, vmem_limit_bytes=56 * 2 ** 20),
            name="tri_stack",
        )(z, m, w_in, w_out, lnp)
        z = z.reshape(CH, R, R, N_DEV).transpose(1, 3, 2, 0).reshape(R, N, CH)
        return lax.all_to_all(z, "dap2", 1, 0, tiled=True)

    return jax.shard_map(local_stack, mesh=mesh, in_specs=(pair_spec, mask_spec, P(), P(), P(), P(), P()), out_specs=pair_spec, check_vma=False)
```

time: 5350 us -> 794 us (0.15)
  waiting for transfers between devices: 2600 us -> 8.52 us
  blocking collectives: 1620 us -> 18.9 us
  Pallas kernels: 0 us -> 727 us
  local copies, waits for them, and re-layouts: 602 us -> 17.6 us
  matrix products: 387 us -> 0 us
  other arithmetic: 87.9 us -> 5.48 us
    all_gather x64 -> x0, waiting for transfers between devices: 2590 us -> none  [the longest x16 1380 us: tri_update(): lax.all_gather(to_transposed(a_proj, row_devs, col_devs), 'dap2', axis=1,...]
    all_to_all x128 -> x1, blocking collectives: 1620 us -> 18.9 us  [local_stack(): return lax.all_to_all(z, 'dap2', 1, 0, tiled=True)]
    pallas_call x0 -> x1, Pallas kernels: none -> 727 us  [local_stack(): pl.pallas_call(functools.partial(body, n_layers), out_shape=jax.ShapeDtyp...]
    all_gather x48 -> x0, local copies, waits for them, and re-layouts: 508 us -> none  [the longest x16 355 us: tri_update(): a_rows = lax.all_gather(a_proj, 'dap2', axis=2, tiled=True)]
    dot_general x128 -> x0, matrix products: 387 us -> none  [the longest x16 120 us: tri_update(): jnp.einsum('cki,ckj->cij', a_cols, b_cols, preferred_element_type=jnp.flo...]
    convert_element_type x73 -> x2, other arithmetic: 63.1 us -> 0.02 us  [the longest x1 0.01 us: local_stack(): lnp = lnp.astype(jnp.float32).reshape(2 * n_layers, CH, 4)]
  transfers between devices with their start and end apart: 64 -> 2, of which waited for: 48 -> 1; matrix products, arithmetic and copies ran while one was open for 5% -> 2% of each run, Pallas kernels for 0% -> 0%
where the time goes in v1:
time: 794 us; the launch traced here: 793 us
  Pallas kernels  727 us (92%)
  blocking collectives  18.9 us (2%)
  local copies, waits for them, and re-layouts  17.6 us (2%)
  starting transfers between devices  15.4 us (2%)
  waiting for transfers between devices  8.52 us (1%)
    pallas_call x1, Pallas kernels, local_stack(): pl.pallas_call(functools.partial(body, n_layers), out_shape=jax.ShapeDtyp...  727 us
    all_to_all x1, blocking collectives, local_stack(): return lax.all_to_all(z, 'dap2', 1, 0, tiled=True)  18.9 us
  transfers between devices with their start and end apart: 2, of which 1 were waited for; matrix products, arithmetic and copies ran while one was open for 2% of the time, Pallas kernels for 0%

profile of v1, /device:TPU:0, one launch (start us, length us, event | category | flops | bytes accessed | tf_op | source)
XLA Modules:
  0.0 793.2 jit_solution(12955153996579159797)
XLA Ops:
  0.0 0.8 copy.55
  0.8 0.6 all_to_all.37
  1.4 8.2 %all-to-all-start.1 = ((s32[16,3,24]{2,1,0:T(4,128)}), s32[16,3,24]{2,1,0:T(4,128)S(1)}, u32[]{:S(2)}, u32[]{:S(2)}) async-start(s32[16,3,24]{2,1,0:T(4,128)} %all_to_all.37), calls=%async_computation.1 | async-start | bytes 65536 | tf_op jit(solution)/shard_map/all_to_all | solution.py:150
  9.6 0.0 copy-start.1
  9.6 5.5 maximum_bitcast_fusion
  15.1 0.0 copy-done.1
  15.1 0.0 copy-start
  15.1 0.0 copy-start.2
  15.2 7.9 copy.58
  23.0 0.0 copy-done
  23.0 1.4 copy.59
  24.4 0.0 all-to-all-done.1
  24.4 7.2 all-to-all-start
  31.7 0.0 copy-done.2
  31.8 2.0 copy.61.lnp
  33.8 0.1 convert_element_type.17
  33.9 0.1 copy.57
  34.0 0.6 convert_element_type.19.mask
  34.6 8.5 %all-to-all-done = f32[48,24,128]{2,1,0:T(8,128)S(1)} async-done(((f32[48,24,128]{2,1,0:T(8,128)}), f32[48,24,128]{2,1,0:T(8,128)S(1)}, u32[]{:S(2)}, u32[]{:S(2)}) %all-to-all-start) | async-done | bytes 589856 | tf_op jit(solution)/shard_map/all_to_all | solution.py:148
  43.2 0.3 reshape.48
  43.5 1.1 copy.60.z_in
  44.6 727.2 %tri_stack.1 = f32[128,1152]{1,0:T(8,128)} custom-call(f32[128,1152]{1,0:T(8,128)} %copy.60.z_in, f32[1,1152]{1,0:T(1,128)} %convert_element_type.19.mask, bf16[32,640,128]{2,1,0:T(8,128)(2,1)} %bitcast.28, bf16[32,128,128]{2,1,0:T(8,128)(2,1)} %bitcast.29, f32[32,128,4]{2,1,0:T(8,128)} %copy.61.lnp), custom_call_target="tpu_custom_call" | custom-call | tf_op jit(solution)/shard_map/tri_stack/pallas_call | solution.py:158
  771.7 1.3 copy.62
  773.0 0.4 copy.67
  773.4 18.9 %all_to_all.46 = f32[3,384,128]{2,0,1:T(4,128)S(1)} all-to-all(f32[3,384,128]{2,0,1:T(4,128)S(1)} %bitcast.30), channel_id=1, replica_groups=mesh['data'=1,'dap2'=16,'dap'=8] {'dap2'}, dimensions={1} | all-to-all | bytes 1179648 | tf_op jit(solution)/shard_map/all_to_all | solution.py:172
  792.4 0.9 copy.66
  (12 shorter events, 0.2 us)
Async XLA Ops:
  1.4 23.0 %all-to-all-start.1 = ((s32[16,3,24]{2,1,0:T(4,128)}), s32[16,3,24]{2,1,0:T(4,128)S(1)}, u32[]{:S(2)}, u32[]{:S(2)}) async-start(s32[16,3,24]{2,1,0:T(4,128)} %all_to_all.37), calls=%async_computation.1 | async-start | bytes 65536 | tf_op jit(solution)/shard_map/all_to_all | solution.py:150
  9.6 5.5 copy-start.1
  15.1 7.9 copy-start
  15.1 16.5 %copy-start.2 = (bf16[16,2,2,128]{3,2,1,0:T(2,128)(2,1)S(1)}, bf16[16,2,2,128]{3,2,1,0:T(2,128)(2,1)}, u32[]{:S(2)}) copy-start(bf16[16,2,2,128]{3,2,1,0:T(2,128)(2,1)} %param.9) | copy-start | bytes 49156
  24.4 18.7 %all-to-all-start = ((f32[48,24,128]{2,1,0:T(8,128)}), f32[48,24,128]{2,1,0:T(8,128)S(1)}, u32[]{:S(2)}, u32[]{:S(2)}) async-start(f32[48,24,128]{2,1,0:T(8,128)} %param.7), calls=%async_computation | async-start | bytes 1179648 | tf_op jit(solution)/shard_map/all_to_all | solution.py:148

commit v2 on v0

v2 whole, which is shorter than its diff:
```python
import functools

import jax
import jax.numpy as jnp
from jax import lax
from jax.experimental import pallas as pl
from jax.experimental.pallas import tpu as pltpu
from jax.sharding import PartitionSpec as P

LN_EPS = 1e-5
N_DEV = 128
CH = 128
N = 384
R = 3
ROWS, COLS = 48, 24
CHUNKS = ((0, 1), (1, 1), (2, 1))
OFFSETS = sorted(((z, y, x, c) for z in (2, 1, 3, 0) for y in (2, 1, 3, 0) for x in (2, 1, 3, 0) for c in (1, 0) if z or y or x or c),
                 key=lambda o: -sum(min(v, 4 - v) for v in o[:3]))


def norm_cols(v, gain, bias):
    mean = jnp.mean(v, axis=0, keepdims=True)
    cen = v - mean
    var = jnp.mean(cen * cen, axis=0, keepdims=True)
    return (cen * lax.rsqrt(var + LN_EPS) * gain + bias).astype(jnp.bfloat16)


def wide(block):
    return jnp.concatenate([block] * 3, axis=1)


def body(n_layers, z_in, m_in, w_ab, w_g, w_o, ln_z, ln_x, z_out,
         zt, zrow, z_blk, mflat, mrow, mask, s_ab, r_ab, s_x, r_x, own_ab, stage, a_mat, b_mat, zn, gate,
         wab_raw, wg_raw, wo_raw, lnz_raw, lnx_raw, w_in, w_out, lnz, lnx,
         sem_sab, sem_rab, sem_sx, sem_rx, sem_w, sem_i, sem_s0, sem_r0, sem_s1, sem_r1, sem_s2, sem_r2):
    d2 = lax.axis_index("dap2")
    d1 = lax.axis_index("dap")
    cz, cy = d2 // 4, d2 % 4
    cx, cc = d1 // 2, d1 % 2
    me = d2 * 8 + d1
    zs, ys = [((cz + d) % 4) * 32 for d in range(4)], [((cy + d) % 4) * 8 for d in range(4)]
    xs = [[((cx + d) % 4) * 2 + (cc + e) % 2 for e in range(2)] for d in range(4)]
    peers = [zs[dz] + ys[dy] + xs[dx][dc] for dz, dy, dx, dc in OFFSETS]

    def dev(t):
        return dict(device_id=t, device_id_type=pl.DeviceIdType.LOGICAL)

    def fetches(u):
        return [pltpu.make_async_copy(src.at[u], dst, sem_w.at[k])
                for k, (src, dst) in enumerate(((w_ab, wab_raw), (w_g, wg_raw), (w_o, wo_raw)))]

    def fetch(u):
        for c in fetches(u):
            c.start()

    def prepare(u, slot):
        for c in fetches(u):
            c.wait()
        w_in[:4 * CH] = wab_raw[...].T
        w_in[4 * CH:] = wg_raw[...].T
        w_out[slot] = wo_raw[...].T
        for k in range(2):
            lnz[k] = jnp.broadcast_to(lnz_raw[u][k:k + 1].astype(jnp.float32), (CH, CH)).T
            lnx[slot, k] = jnp.broadcast_to(lnx_raw[u][k:k + 1].astype(jnp.float32), (CH, CH)).T

    fetch(0)
    firsts = [pltpu.make_async_copy(src, dst, sem_i.at[k])
              for k, (src, dst) in enumerate(((z_in, z_blk), (ln_z, lnz_raw), (ln_x, lnx_raw)))]
    for c in firsts:
        c.start()
    bar = pltpu.get_barrier_semaphore()
    for t in peers:
        pl.semaphore_signal(bar, inc=1, **dev(t))

    my_cols = pl.ds(pl.multiple_of(COLS * d2, 8), COLS)
    my_mask = pl.ds(3 * d2, 3)
    pad = jnp.concatenate([m_in[...].astype(jnp.float32), jnp.zeros((ROWS, N - COLS), jnp.float32)], axis=1)
    pad = pltpu.roll(pad, COLS * d2, 1)
    for t in range(3):
        mflat[pl.ds(t, ROWS, stride=3), :] = pad[:, t * 128:(t + 1) * 128]
    for c in firsts:
        c.wait()
    prepare(0, 0)
    pl.semaphore_wait(bar, N_DEV - 1)

    def block_rows(fn):
        def one(k, carry):
            ii = (k + R * d2) % ROWS
            i = ROWS * d1 + ii
            fn(ii, i % N_DEV, i // N_DEV)
            return carry
        lax.fori_loop(0, ROWS, one, 0)

    def move(src, dst, sem_s, sem_r, t):
        @pl.when(t == me)
        def _():
            dst[...] = src[...]

        @pl.when(t != me)
        def _():
            pltpu.make_async_remote_copy(src_ref=src, dst_ref=dst, send_sem=sem_s, recv_sem=sem_r, **dev(t)).start()

    def take(ref, unit, count, sem, but_one):
        for n, when in ((count - 1, but_one), (count, jnp.logical_not(but_one))):
            @pl.when(when)
            def _():
                some = ref.at[pl.ds(0, n * unit)]
                pltpu.make_async_copy(some, some, sem).wait()

    stays = (me + N_DEV * R - ROWS * d1) % N_DEV < ROWS

    def scatter(ii, g, r):
        move(z_blk.at[ii], zrow.at[r, my_cols], sem_s0, sem_r0.at[r], g)
        move(mflat.at[pl.ds(3 * ii, 3)], mrow.at[r, my_mask], sem_s1, sem_r1.at[r], g)

    block_rows(scatter)

    def toks(r):
        return pl.ds(pl.multiple_of(r * N, 128), N)

    def load_state(r):
        own = (me + N_DEV * r) // ROWS == d1
        take(zrow.at[r], COLS, 16, sem_r0.at[r], own)
        take(mrow.at[r], 3, 16, sem_r1.at[r], own)
        zt[:, toks(r)] = zrow[r].T
        for t in range(3):
            mask[r, :, t * 128:(t + 1) * 128] = jnp.sum(mrow[r, pl.ds(t, 16, stride=3), :], axis=0, keepdims=True)

    def part(ref, c, rows):
        r0, n = CHUNKS[c]
        return ref.at[r0, rows] if n == 1 else ref.at[pl.ds(r0, n), rows]

    def send(src, dst, rows, sem_s, sem_r, c):
        mine = part(dst, c, pl.ds(me * rows, rows))
        for t in peers:
            pltpu.make_async_remote_copy(src_ref=part(src, c, pl.ds(t * rows, rows)), dst_ref=mine,
                                         send_sem=sem_s.at[c], recv_sem=sem_r.at[c], **dev(t)).start()

    def wait(src, dst, rows, sem, c):
        most = pl.ds(0, rows * (N_DEV - 1))
        pltpu.make_async_copy(part(src, c, most), part(dst, c, most), sem.at[c]).wait()

    def rows_of(c, fn):
        r0, n = CHUNKS[c]
        if n == 1:
            fn(r0)
        else:
            def one(k, carry):
                fn(r0 + k)
                return carry
            lax.fori_loop(0, n, one, 0)

    def project(r):
        n = norm_cols(zt[:, toks(r)], wide(lnz[0]), wide(lnz[1]))
        zn[:, toks(r)] = n
        q = jnp.dot(w_in[:4 * CH], n, preferred_element_type=jnp.float32)
        m = mask[r]
        a = m * jax.nn.sigmoid(q[CH:2 * CH]) * q[:CH]
        b = m * jax.nn.sigmoid(q[3 * CH:]) * q[2 * CH:3 * CH]
        for kh in range(3):
            stage[pl.ds(2 * kh, CH, stride=6), :] = a[:, kh * 128:(kh + 1) * 128]
            stage[pl.ds(2 * kh + 1, CH, stride=6), :] = b[:, kh * 128:(kh + 1) * 128]
        own_ab[r, 0:6] = stage[pl.ds(6 * me, 6), :].astype(jnp.bfloat16).astype(jnp.float32)
        s_ab[r] = stage[...].astype(jnp.bfloat16)

    def gates():
        def one(r, carry):
            gate[:, toks(r)] = jax.nn.sigmoid(jnp.dot(w_in[4 * CH:], zn[:, toks(r)], preferred_element_type=jnp.float32))
            return carry
        lax.fori_loop(0, R, one, 0)

    def gather_mats(r):
        stage[...] = r_ab[r].astype(jnp.float32)
        stage[pl.ds(6 * me, 6), :] = own_ab[r, 0:6]
        row = pl.ds(pl.multiple_of(r * 128, 128), 128)
        for kh in range(3):
            a_mat[row, kh * 128:(kh + 1) * 128] = stage[pl.ds(2 * kh, 128, stride=6), :].astype(jnp.bfloat16)
            b_mat[row, kh * 128:(kh + 1) * 128] = stage[pl.ds(2 * kh + 1, 128, stride=6), :].astype(jnp.bfloat16)

    def contract(outgoing, r):
        row = pl.ds(pl.multiple_of(r * 128, 128), 128)
        if outgoing:
            x = lax.dot_general(a_mat[row, :], b_mat[...], (((1,), (1,)), ((), ())), preferred_element_type=jnp.float32)
        else:
            x = lax.dot_general(a_mat[:, row], b_mat[...], (((0,), (0,)), ((), ())), preferred_element_type=jnp.float32)
        for jh in range(3):
            s_x[r, pl.ds(jh, 128, stride=3), :] = x[:, jh * 128:(jh + 1) * 128]

    def finish(slot, r):
        r_x[r, pl.ds(3 * me, 3), :] = s_x[r, pl.ds(3 * me, 3), :]
        x = jnp.concatenate([r_x[r, pl.ds(jh, CH, stride=3), :] for jh in range(3)], axis=1)
        xn = norm_cols(x, wide(lnx[slot, 0]), wide(lnx[slot, 1]))
        y = jnp.dot(w_out[slot], xn, preferred_element_type=jnp.float32)
        zt[:, toks(r)] = zt[:, toks(r)] + gate[:, toks(r)] * y

    def leave(r):
        zrow[r] = zt[:, toks(r)].T
        i = me + N_DEV * r
        for k in range(16):
            b = (d2 + k) % 16
            move(zrow.at[r, pl.ds(pl.multiple_of(b * COLS, 8), COLS)], z_out.at[i % ROWS], sem_s2, sem_r2, b * 8 + i // ROWS)

    n_chunks = len(CHUNKS)

    def spread(outgoing):
        for c in range(n_chunks):
            wait(s_ab, r_ab, 6, sem_rab, c)
            rows_of(c, gather_mats)
        for c in range(n_chunks):
            rows_of(c, lambda r: contract(outgoing, r))
            send(s_x, r_x, 3, sem_sx, sem_rx, c)

    def collect(slot, c):
        wait(s_x, r_x, 3, sem_rx, c)
        rows_of(c, lambda r: finish(slot, r))
        wait(s_x, r_x, 3, sem_sx, c)

    def emit(c, first):
        if not first:
            wait(s_ab, r_ab, 6, sem_sab, c)
        rows_of(c, project)
        send(s_ab, r_ab, 6, sem_sab, sem_rab, c)

    for c in range(n_chunks):
        rows_of(c, load_state)
        emit(c, True)
    gates()

    take(z_blk, 1, ROWS, sem_s0, stays)
    take(mflat, 3, ROWS, sem_s1, stays)

    def layer(l, carry):
        fetch(2 * l + 1)
        spread(True)
        prepare(2 * l + 1, 1)
        for c in range(n_chunks):
            collect(0, c)
            emit(c, False)
        gates()
        more = l < n_layers - 1

        @pl.when(more)
        def _():
            fetch(2 * l + 2)
        spread(False)

        @pl.when(more)
        def _():
            prepare(2 * l + 2, 0)
        for c in range(n_chunks):
            collect(1, c)

            @pl.when(more)
            def _():
                emit(c, False)

            @pl.when(l == n_layers - 1)
            def _():
                rows_of(c, leave)

        @pl.when(more)
        def _():
            gates()
        return carry

    lax.fori_loop(0, n_layers, layer, 0)
    for c in range(n_chunks):
        wait(s_ab, r_ab, 6, sem_sab, c)

    take(z_out, 1, ROWS, sem_s2, stays)
    take(z_out, 1, ROWS, sem_r2, stays)


def solution(mesh):
    pair_spec = P(("data", "dap"), "dap2", None)
    mask_spec = P(("data", "dap"), "dap2")

    def local_stack(pair_act, pair_mask, ln_z, w_ab, w_g, ln_x, w_o):
        n_layers = w_o.shape[0]
        run_layers = n_layers
        vmem, hbm = pl.BlockSpec(memory_space=pltpu.VMEM), pl.BlockSpec(memory_space=pltpu.HBM)
        f32, bf16 = jnp.float32, jnp.bfloat16
        dma, dmas = pltpu.SemaphoreType.DMA, pltpu.SemaphoreType.DMA((R,))
        scratch = [
            ((CH, R * N), f32), ((R, N, CH), f32), (pair_act.shape, f32), ((R * ROWS, 128), f32), ((R, 3 * 16, 128), f32), ((R, 1, N), f32),
            ((R, 6 * N_DEV, 128), bf16), ((R, 6 * N_DEV, 128), bf16), ((R, 3 * N_DEV, 128), f32), ((R, 3 * N_DEV, 128), f32),
            ((R, 8, 128), f32), ((6 * N_DEV, 128), f32), ((N, N), bf16), ((N, N), bf16), ((CH, R * N), bf16), ((CH, R * N), f32),
            ((CH, 4 * CH), bf16), ((CH, CH), bf16), ((CH, CH), bf16), ((2 * n_layers, 2, CH), bf16), ((2 * n_layers, 2, CH), bf16), ((5 * CH, CH), bf16), ((2, CH, CH), bf16),
            ((2, CH, CH), f32), ((2, 2, CH, CH), f32)]
        return pl.pallas_call(
            functools.partial(body, run_layers),
            out_shape=jax.ShapeDtypeStruct(pair_act.shape, f32),
            in_specs=[hbm, vmem, hbm, hbm, hbm, hbm, hbm], out_specs=vmem,
            scratch_shapes=[pltpu.VMEM(s, t) for s, t in scratch] + [dmas] * 6 + [dma, dmas, dma, dmas, dma, dma],
            compiler_params=pltpu.CompilerParams(collective_id=0, has_side_effects=True, vmem_limit_bytes=67043328 - 800 * 1024),
            name="tri_stack",
        )(pair_act, pair_mask, w_ab.reshape(2 * n_layers, CH, 4 * CH), w_g.reshape(2 * n_layers, CH, CH),
          w_o.reshape(2 * n_layers, CH, CH), ln_z.reshape(2 * n_layers, 2, CH), ln_x.reshape(2 * n_layers, 2, CH))

    return jax.shard_map(local_stack, mesh=mesh, in_specs=(pair_spec, mask_spec, P(), P(), P(), P(), P()), out_specs=pair_spec, check_vma=False)
```

time: 5350 us -> 617 us (0.12)
  waiting for transfers between devices: 2600 us -> 0 us
  blocking collectives: 1620 us -> 0 us
  Pallas kernels: 0 us -> 612 us
  local copies, waits for them, and re-layouts: 602 us -> 3.31 us
  matrix products: 387 us -> 0 us
  other arithmetic: 87.9 us -> 0 us
    all_gather x64 -> x0, waiting for transfers between devices: 2590 us -> none  [the longest x16 1380 us: tri_update(): lax.all_gather(to_transposed(a_proj, row_devs, col_devs), 'dap2', axis=1,...]
    all_to_all x128 -> x0, blocking collectives: 1620 us -> none  [the longest x32 439 us: to_transposed(): stage_one = lax.all_to_all(blocks, 'dap2', 1, 2, tiled=True)]
    pallas_call x0 -> x1, Pallas kernels: none -> 612 us  [local_stack(): pl.pallas_call(functools.partial(body, run_layers), out_shape=jax.ShapeDt...]
    all_gather x48 -> x0, local copies, waits for them, and re-layouts: 508 us -> none  [the longest x16 355 us: tri_update(): a_rows = lax.all_gather(a_proj, 'dap2', axis=2, tiled=True)]
    dot_general x128 -> x0, matrix products: 387 us -> none  [the longest x16 120 us: tri_update(): jnp.einsum('cki,ckj->cij', a_cols, b_cols, preferred_element_type=jnp.flo...]
    convert_element_type x73 -> x0, other arithmetic: 63.1 us -> none  [the longest x32 34.8 us: project_local(): (keep_mask * jax.nn.sigmoid(projected[3 * hidden:]) * projected[2 * hidde...]
  transfers between devices with their start and end apart: 64 -> 0, of which waited for: 48 -> 0; matrix products, arithmetic and copies ran while one was open for 5% -> 0% of each run, Pallas kernels for 0% -> 0%
where the time goes in v2:
time: 617 us; the launch traced here: 615 us
  Pallas kernels  612 us (99%)
    pallas_call x1, Pallas kernels, local_stack(): pl.pallas_call(functools.partial(body, run_layers), out_shape=jax.ShapeDt...  612 us

profile of v2, /device:TPU:0, one launch (start us, length us, event | category | flops | bytes accessed | tf_op | source)
XLA Modules:
  0.0 614.9 jit_solution(14507556365705300680)
XLA Ops:
  0.0 1.4 copy.8.m_in
  1.4 611.5 %tri_stack.1 = f32[48,24,128]{2,1,0:T(8,128)} custom-call(f32[48,24,128]{2,1,0:T(8,128)} %z_in.1, s32[48,24]{1,0:T(8,128)} %copy.8.m_in, bf16[32,128,512]{2,1,0:T(8,128)(2,1)} %bitcast.5, bf16[32,128,128]{2,1,0:T(8,128)(2,1)} %bitcast.6, bf16[32,128,128]{2,1,0:T(8,128)(2,1)} %bitcast.7, bf16[32,2,128]{2,1,0:T(2,128)(2,1)} %bitcast.8, bf16[32,2,128]{2,1,0:T(2,128)(2,1)} %bitcast.9), custom_call_target="tpu_custom_call" | custom-call | tf_op jit(solution)/shard_map/tri_stack/pallas_call | solution.py:290
  612.9 1.9 copy.10
